TPU v7x, 32 devices: a 4x4x1 block of a 4x4x8 slice. The times are simulated.
32 devices in a mesh: inst: 1 (over z), qy: 4 (over y), qx: 8 (over x, core).
Axes of the slice: x: 4, y: 4, z: 1, core: 2. Of those that a mesh axis runs over, the one named last changes fastest.
The devices are a block of a 4x4x8 slice.
Arguments:
- cost_diag: float32 [262144], P(('inst', 'qx', 'qy'))
- gamma_angles: float32 [4], replicated
- beta_angles: float32 [4], replicated
Outputs:
- output 1: float32 [1], P('inst')
- output 2: float32 [262144], P(('inst', 'qx', 'qy'))
- output 3: float32 [262144], P(('inst', 'qx', 'qy'))
All inputs are finite; a program needn't handle non-finite values.
Results may differ from a plain program's by a relative error of at most 0.001.
Values sent between devices are 32-bit elements.
A program may use at most 768 MiB of HBM per device.

v0:
```python
import functools
import math
import jax
import jax.numpy as jnp
from jax import lax
from jax.experimental import pallas as pl
from jax.experimental.pallas import tpu as pltpu
from jax.sharding import PartitionSpec as P

LANES = 128
SIN_POLY = (4.442883014678955, -7.308245658874512, 3.606354236602783, -0.8461116552352905, 0.1098245158791542)
COS_POLY = (1.4142135381698608, -6.9788641929626465, 5.73988151550293, -1.888274908065796, 0.33225154876708984, -0.034501612186431885)
F32 = jnp.float32
BF16 = jnp.bfloat16


def flip_bits(value, mask):
    bit = 1
    while bit <= mask:
        if mask & bit:
            value = value + bit * (1 - 2 * ((value // bit) % 2))
        bit *= 2
    return value


def turn_cos_sin(turns):
    rem = turns - jnp.round(turns)
    sq = rem * rem
    s = SIN_POLY[-1]
    for k in SIN_POLY[-2::-1]:
        s = s * sq + k
    s = s * rem
    c = COS_POLY[-1]
    for k in COS_POLY[-2::-1]:
        c = c * sq + k
    return 1.0 - s * s, s * c


def split3(x):
    a = x.astype(BF16)
    r = x - a.astype(F32)
    b = r.astype(BF16)
    c = (r - b.astype(F32)).astype(BF16)
    return a, b, c


def dot6_lhs(lhs_parts, rhs_cat):
    a, b, c = lhs_parts
    return jnp.dot(jnp.concatenate([a, a, b, a, b, c], axis=1), rhs_cat, preferred_element_type=F32)


def exchange_kernel(half, nqy, cost_ref, table_ref, packet, send_sem, recv_sem):
    me_x, me_y = lax.axis_index('qx'), lax.axis_index('qy')
    barrier = pltpu.get_barrier_semaphore()

    def partner(e):
        return {'qx': flip_bits(me_x, e // nqy), 'qy': flip_bits(me_y, e % nqy)}

    for e in range(1, half):
        pl.semaphore_signal(barrier, inc=1, device_id=partner(e), device_id_type=pl.DeviceIdType.MESH)
    rows = cost_ref.shape[0]
    cost = cost_ref[...]
    rev = reverse_rows(cost)
    col = jnp.concatenate([cost, rev], axis=0).T[0:1, :]
    pk = jnp.concatenate([cost[0:1, :], col, jnp.zeros((6, LANES), F32)], axis=0)
    packet[...] = pk
    table_ref[0, :, :] = pk
    pl.semaphore_wait(barrier, half - 1)
    copies = []
    for e in range(1, half):
        copy = pltpu.make_async_remote_copy(
            src_ref=packet.at[0:2], dst_ref=table_ref.at[e, 0:2], send_sem=send_sem.at[e], recv_sem=recv_sem.at[e],
            device_id=partner(e), device_id_type=pl.DeviceIdType.MESH)
        copy.start()
        copies.append(copy)
    for copy in copies:
        copy.wait()


def reverse_rows(x):
    n = x.shape[0]
    i = lax.broadcasted_iota(jnp.int32, (n, n), 0)
    j = lax.broadcasted_iota(jnp.int32, (n, n), 1)
    perm = jnp.where(i + j == n - 1, 1.0, 0.0).astype(F32)
    return jnp.dot(perm, x, precision=lax.Precision.HIGHEST, preferred_element_type=F32)


def product_matrix(diag, off0, off1, scale):
    lane = lax.broadcasted_iota(jnp.int32, (8, LANES), 1)
    sub = lax.broadcasted_iota(jnp.int32, (8, LANES), 0)
    bit = lambda v, b: (v // (1 << b)) % 2
    base = jnp.full((8, LANES), 1.0, F32) * scale
    rows = [[None, None] for _ in range(7)]
    for b in range(7):
        lb = bit(lane, b) == 1
        row0 = jnp.where(lb, off0, diag[0])
        row1 = jnp.where(lb, diag[1], off1)
        rows[b] = [row0, row1]
    for b in range(3):
        base = base * jnp.where(bit(sub, b) == 1, rows[b][1], rows[b][0])
    blocks = [base]
    for b in range(3, 7):
        blocks = [x * rows[b][0] for x in blocks] + [x * rows[b][1] for x in blocks]
    return jnp.concatenate(blocks, axis=0)


def simulate_kernel(layers, total_bits, gamma_ref, beta_ref, cost_ref, table_ref, energy_ref, re_ref, im_ref,
                    cst, sre, sim):
    rows = cost_ref.shape[0]
    cost = cost_ref[...]
    rev = reverse_rows(cost)
    first = jnp.concatenate([table_ref[e, 0:1, :] - cost[0:1, :] for e in range(16)], axis=0)
    own_col = table_ref[0, 1:2, :]
    cols = jnp.concatenate([table_ref[e, 1:2, :] - own_col for e in range(16)], axis=0)
    cols = cols - cols[:, 0:1]
    cols_t = jnp.concatenate([cols, jnp.zeros((LANES - 16, LANES), F32)], axis=0).T
    for t in range(2):
        for u in range(4):
            for e0s in range(2):
                e = t * 8 + u * 2 + (e0s ^ t)
                base = rev if t else cost
                cst[t, u, e0s * rows:(e0s + 1) * rows, :] = base + (first[e:e + 1, :] + cols_t[t * rows:(t + 1) * rows, e:e + 1])

    lane = lax.broadcasted_iota(jnp.int32, (LANES, LANES), 1)
    vrow = lax.broadcasted_iota(jnp.int32, (LANES, LANES), 0)
    ones = jnp.zeros((LANES, LANES), jnp.int32)
    for b in range(7):
        ones = ones + (lane // (1 << b)) % 2 + (vrow // (1 << b)) % 2
    quarter = (ones % 4).astype(F32) * 0.25

    amp = 2.0 ** (-total_bits / 2.0)
    for l in range(layers):
        g = gamma_ref[l] * (1.0 / (2.0 * math.pi))
        half_beta = jnp.full((8, LANES), 0.5, F32) * beta_ref[l]
        c, s = jnp.cos(half_beta), jnp.sin(half_beta)
        rot = product_matrix((c, c), -s, s, c)
        rot_t = product_matrix((c, c), s, -s, c)
        rk = product_matrix((-s, -s), -c, c, -s)
        rk_t = product_matrix((-s, -s), c, -c, -s)
        w = jnp.concatenate([jnp.concatenate([rot, rk], axis=1), jnp.concatenate([rk, rot], axis=1)], axis=0)
        m = jnp.concatenate([jnp.concatenate([rot_t, rk_t], axis=1), jnp.concatenate([rk_t, rot_t], axis=1)], axis=0)
        w1, w2, w3 = split3(w)
        wcat = jnp.concatenate([w1, w1, w2, w1, w2, w3], axis=1)
        m1, m2, m3 = split3(m)
        mcat = jnp.concatenate([m1, m2, m1, m3, m2, m1], axis=0)
        c2, s2, sc = (c * c)[0:1, :], (s * s)[0:1, :], (s * c)[0:1, :]
        ys = []
        for u in range(4):
            parts = []
            for t in range(2):
                turns = cst[t, u] * g
                if l == 0:
                    turns = turns - jnp.round(turns) - quarter
                    co, si = turn_cos_sin(turns)
                    re, im = amp * co, -amp * si
                else:
                    co, si = turn_cos_sin(turns)
                    a, b = sre[t, u], sim[t, u]
                    re, im = a * co + b * si, b * co - a * si
                parts.append(jnp.concatenate([re, im], axis=1))
            x1, x2, x3 = split3(jnp.concatenate(parts, axis=0))
            xcat = jnp.concatenate([x1, x2, x1, x3, x2, x1], axis=0)
            ys.append(jnp.dot(wcat, xcat, preferred_element_type=F32))
        zs = {}
        for u in range(4):
            y0, y1 = ys[u], ys[3 - u]
            lhs = jnp.concatenate([
                jnp.concatenate([y0[:LANES, :LANES], y1[LANES:, :LANES]], axis=1),
                jnp.concatenate([y0[:LANES, LANES:], y1[LANES:, LANES:]], axis=1)], axis=0)
            z = dot6_lhs(split3(lhs), mcat)
            zs[0, u] = (z[:LANES, :LANES], z[LANES:, :LANES])
            zs[1, 3 - u] = (z[:LANES, LANES:], z[LANES:, LANES:])
        for t in range(2):
            zr = [zs[t, u][0] for u in range(4)]
            zi = [zs[t, u][1] for u in range(4)]
            br = [sc * (zi[1] + zi[2]), sc * (zi[0] + zi[3])]
            bi = [sc * (zr[1] + zr[2]), sc * (zr[0] + zr[3])]
            for u in range(4):
                k = 0 if u in (0, 3) else 1
                sre[t, u] = c2 * zr[u] - s2 * zr[3 - u] + br[k]
                sim[t, u] = c2 * zi[u] - s2 * zi[3 - u] - bi[k]

    total = jnp.zeros((LANES, LANES), F32)
    for t in range(2):
        for u in range(4):
            a, b = sre[t, u], sim[t, u]
            total = total + cst[t, u] * (a * a + b * b)
    energy_ref[...] = jnp.full((8, LANES), 2.0 * jnp.sum(total), F32)
    a, b = sre[0, 0, 0:rows, :], sim[0, 0, 0:rows, :]
    k = ones[0:rows, :] % 4
    re_ref[...] = jnp.where(k == 0, a, jnp.where(k == 1, b, jnp.where(k == 2, -a, -b)))
    im_ref[...] = jnp.where(k == 0, b, jnp.where(k == 1, -a, jnp.where(k == 2, -b, a)))


def solution(mesh):
    nqx, nqy = mesh.shape['qx'], mesh.shape['qy']
    half = nqx * nqy // 2
    state_spec = P(('inst', 'qx', 'qy'))
    vmem = pl.BlockSpec(memory_space=pltpu.VMEM)
    smem = pl.BlockSpec(memory_space=pltpu.SMEM)

    def device_body(cost_loc, gamma_angles, beta_angles):
        local = cost_loc.shape[0]
        rows = local // LANES
        total_bits = int(math.log2(local * nqx * nqy))
        layers = gamma_angles.shape[0]
        cost2 = cost_loc.reshape(rows, LANES)
        table = pl.pallas_call(
            functools.partial(exchange_kernel, half, nqy),
            out_shape=jax.ShapeDtypeStruct((half, 8, LANES), F32),
            in_specs=[vmem], out_specs=vmem,
            scratch_shapes=[pltpu.VMEM((8, LANES), F32), pltpu.SemaphoreType.DMA((half,)), pltpu.SemaphoreType.DMA((half,))],
            compiler_params=pltpu.CompilerParams(collective_id=0, has_side_effects=True),
        )(cost2)
        st = jax.ShapeDtypeStruct((rows, LANES), F32)
        energy, re, im = pl.pallas_call(
            functools.partial(simulate_kernel, layers, total_bits),
            out_shape=(jax.ShapeDtypeStruct((8, LANES), F32), st, st),
            in_specs=[smem, smem, vmem, vmem], out_specs=(vmem, vmem, vmem),
            scratch_shapes=[pltpu.VMEM((2, 4, LANES, LANES), F32)] * 3,
        )(gamma_angles, beta_angles, cost2, table)
        return energy[0, 0:1], re.reshape(local), im.reshape(local)

    return jax.shard_map(device_body, mesh=mesh, in_specs=(state_spec, P(), P()), out_specs=(P('inst'), state_spec, state_spec), check_vma=False)
```

profile of v0, /device:TPU:97, one launch (start us, length us, event | category | flops | bytes accessed | tf_op | source)
XLA Modules:
  0.0 24.5 jit_solution(15941705621820161019)
XLA Ops:
  0.6 11.5 %shard_map.58.table_ref = f32[16,8,128]{2,1,0:T(8,128)} custom-call(f32[64,128]{1,0:T(8,128)} %bitcast.4), custom_call_target="tpu_custom_call" | custom-call | tf_op jit(solution)/shard_map/pallas_call | solution.py:208
  12.1 11.2 %shard_map.59 = (f32[8,128]{1,0:T(8,128)}, f32[64,128]{1,0:T(8,128)}, f32[64,128]{1,0:T(8,128)}) custom-call(f32[4]{0:T(128)} %gamma_ref.1, f32[4]{0:T(128)} %beta_ref.1, f32[64,128]{1,0:T(8,128)} %bitcast.5, f32[16,8,128]{2,1,0:T(8,128)} %shard_map.58.table_ref), custom_call_target="tpu_custom_call" | custom-call | tf_op jit(solution)/shard_map/pallas_call | solution.py:216
  23.3 1.2 %slice.3 = f32[1,1]{1,0:T(1,128)} slice(f32[8,128]{1,0:T(8,128)} %get-tuple-element.6), slice={[0:1], [0:1]} | slice | bytes 8 | tf_op jit(solution)/shard_map/slice | solution.py:222
where the time goes:
time: 24.7 us; the launch traced here: 24.5 us
  Pallas kernels  22.7 us (92%)
  local copies, waits for them, and re-layouts  1.19 us (5%)
  between operations  0.64 us (3%)
    pallas_call x1, Pallas kernels, device_body(): pl.pallas_call(functools.partial(exchange_kernel, half, nqy), out_shape=j...  11.5 us
    pallas_call x1, Pallas kernels, device_body(): pl.pallas_call(functools.partial(simulate_kernel, layers, total_bits), ou...  11.2 us
    slice x1, local copies, waits for them, and re-layouts, device_body(): return (energy[0, 0:1], re.reshape(local), im.reshape(local))  1.19 us

commit v1 on v0

--- a/solution.py
+++ b/solution.py
@@ -47,34 +47,6 @@
 def dot6_lhs(lhs_parts, rhs_cat):
     a, b, c = lhs_parts
     return jnp.dot(jnp.concatenate([a, a, b, a, b, c], axis=1), rhs_cat, preferred_element_type=F32)
-
-
-def exchange_kernel(half, nqy, cost_ref, table_ref, packet, send_sem, recv_sem):
-    me_x, me_y = lax.axis_index('qx'), lax.axis_index('qy')
-    barrier = pltpu.get_barrier_semaphore()
-
-    def partner(e):
-        return {'qx': flip_bits(me_x, e // nqy), 'qy': flip_bits(me_y, e % nqy)}
-
-    for e in range(1, half):
-        pl.semaphore_signal(barrier, inc=1, device_id=partner(e), device_id_type=pl.DeviceIdType.MESH)
-    rows = cost_ref.shape[0]
-    cost = cost_ref[...]
-    rev = reverse_rows(cost)
-    col = jnp.concatenate([cost, rev], axis=0).T[0:1, :]
-    pk = jnp.concatenate([cost[0:1, :], col, jnp.zeros((6, LANES), F32)], axis=0)
-    packet[...] = pk
-    table_ref[0, :, :] = pk
-    pl.semaphore_wait(barrier, half - 1)
-    copies = []
-    for e in range(1, half):
-        copy = pltpu.make_async_remote_copy(
-            src_ref=packet.at[0:2], dst_ref=table_ref.at[e, 0:2], send_sem=send_sem.at[e], recv_sem=recv_sem.at[e],
-            device_id=partner(e), device_id_type=pl.DeviceIdType.MESH)
-        copy.start()
-        copies.append(copy)
-    for copy in copies:
-        copy.wait()
 
 
 def reverse_rows(x):
@@ -104,33 +76,35 @@
     return jnp.concatenate(blocks, axis=0)
 
 
-def simulate_kernel(layers, total_bits, gamma_ref, beta_ref, cost_ref, table_ref, energy_ref, re_ref, im_ref,
-                    cst, sre, sim):
+def kernel(layers, total_bits, half, nqy, gamma_ref, beta_ref, cost_hbm, energy_ref, re_ref, im_ref,
+           cost_ref, table_ref, packet, cst, sre, sim, wcat_ref, mcat_ref, load_sem, send_sem, recv_sem):
+    load = pltpu.make_async_copy(cost_hbm, cost_ref, load_sem)
+    load.start()
+    me_x, me_y = lax.axis_index('qx'), lax.axis_index('qy')
+    barrier = pltpu.get_barrier_semaphore()
+
+    def partner(e):
+        return {'qx': flip_bits(me_x, e // nqy), 'qy': flip_bits(me_y, e % nqy)}
+
+    for e in range(1, half):
+        pl.semaphore_signal(barrier, inc=1, device_id=partner(e), device_id_type=pl.DeviceIdType.MESH)
+    load.wait()
     rows = cost_ref.shape[0]
     cost = cost_ref[...]
     rev = reverse_rows(cost)
-    first = jnp.concatenate([table_ref[e, 0:1, :] - cost[0:1, :] for e in range(16)], axis=0)
-    own_col = table_ref[0, 1:2, :]
-    cols = jnp.concatenate([table_ref[e, 1:2, :] - own_col for e in range(16)], axis=0)
-    cols = cols - cols[:, 0:1]
-    cols_t = jnp.concatenate([cols, jnp.zeros((LANES - 16, LANES), F32)], axis=0).T
-    for t in range(2):
-        for u in range(4):
-            for e0s in range(2):
-                e = t * 8 + u * 2 + (e0s ^ t)
-                base = rev if t else cost
-                cst[t, u, e0s * rows:(e0s + 1) * rows, :] = base + (first[e:e + 1, :] + cols_t[t * rows:(t + 1) * rows, e:e + 1])
-
-    lane = lax.broadcasted_iota(jnp.int32, (LANES, LANES), 1)
-    vrow = lax.broadcasted_iota(jnp.int32, (LANES, LANES), 0)
-    ones = jnp.zeros((LANES, LANES), jnp.int32)
-    for b in range(7):
-        ones = ones + (lane // (1 << b)) % 2 + (vrow // (1 << b)) % 2
-    quarter = (ones % 4).astype(F32) * 0.25
-
-    amp = 2.0 ** (-total_bits / 2.0)
+    col = jnp.concatenate([cost, rev], axis=0).T[0:1, :]
+    packet[0:1, :] = cost[0:1, :]
+    packet[1:2, :] = col
+    pl.semaphore_wait(barrier, half - 1)
+    copies = []
+    for e in range(1, half):
+        copy = pltpu.make_async_remote_copy(
+            src_ref=packet.at[0:2], dst_ref=table_ref.at[e, 0:2], send_sem=send_sem.at[e], recv_sem=recv_sem.at[e],
+            device_id=partner(e), device_id_type=pl.DeviceIdType.MESH)
+        copy.start()
+        copies.append(copy)
+    trig = []
     for l in range(layers):
-        g = gamma_ref[l] * (1.0 / (2.0 * math.pi))
         half_beta = jnp.full((8, LANES), 0.5, F32) * beta_ref[l]
         c, s = jnp.cos(half_beta), jnp.sin(half_beta)
         rot = product_matrix((c, c), -s, s, c)
@@ -139,11 +113,41 @@
         rk_t = product_matrix((-s, -s), c, -c, -s)
         w = jnp.concatenate([jnp.concatenate([rot, rk], axis=1), jnp.concatenate([rk, rot], axis=1)], axis=0)
         m = jnp.concatenate([jnp.concatenate([rot_t, rk_t], axis=1), jnp.concatenate([rk_t, rot_t], axis=1)], axis=0)
-        w1, w2, w3 = split3(w)
+        for k, part in enumerate(split3(w)):
+            wcat_ref[l, k] = part
+        for k, part in enumerate(split3(m)):
+            mcat_ref[l, k] = part
+        trig.append(((c * c)[0:1, :], (s * s)[0:1, :], (s * c)[0:1, :]))
+
+    lane = lax.broadcasted_iota(jnp.int32, (LANES, LANES), 1)
+    vrow = lax.broadcasted_iota(jnp.int32, (LANES, LANES), 0)
+    ones = jnp.zeros((LANES, LANES), jnp.int32)
+    for b in range(7):
+        ones = ones + (lane // (1 << b)) % 2 + (vrow // (1 << b)) % 2
+    quarter = (ones % 4).astype(F32) * 0.25
+
+    for copy in copies:
+        copy.wait()
+    first = jnp.concatenate([(table_ref[e, 0:1, :] - cost[0:1, :]) if e else jnp.zeros((1, LANES), F32) for e in range(16)], axis=0)
+    own_col = col
+    cols = jnp.concatenate([(table_ref[e, 1:2, :] - own_col) if e else jnp.zeros((1, LANES), F32) for e in range(16)], axis=0)
+    cols = cols - cols[:, 0:1]
+    cols_t = jnp.concatenate([cols, jnp.zeros((LANES - 16, LANES), F32)], axis=0).T
+    for t in range(2):
+        for u in range(4):
+            for e0s in range(2):
+                e = t * 8 + u * 2 + (e0s ^ t)
+                base = rev if t else cost
+                cst[t, u, e0s * rows:(e0s + 1) * rows, :] = base + (first[e:e + 1, :] + cols_t[t * rows:(t + 1) * rows, e:e + 1])
+
+    amp = 2.0 ** (-total_bits / 2.0)
+    for l in range(layers):
+        g = gamma_ref[l] * (1.0 / (2.0 * math.pi))
+        w1, w2, w3 = [wcat_ref[l, k] for k in range(3)]
         wcat = jnp.concatenate([w1, w1, w2, w1, w2, w3], axis=1)
-        m1, m2, m3 = split3(m)
+        m1, m2, m3 = [mcat_ref[l, k] for k in range(3)]
         mcat = jnp.concatenate([m1, m2, m1, m3, m2, m1], axis=0)
-        c2, s2, sc = (c * c)[0:1, :], (s * s)[0:1, :], (s * c)[0:1, :]
+        c2, s2, sc = trig[l]
         ys = []
         for u in range(4):
             parts = []
@@ -185,7 +189,7 @@
         for u in range(4):
             a, b = sre[t, u], sim[t, u]
             total = total + cst[t, u] * (a * a + b * b)
-    energy_ref[...] = jnp.full((8, LANES), 2.0 * jnp.sum(total), F32)
+    energy_ref[0] = 2.0 * jnp.sum(total)
     a, b = sre[0, 0, 0:rows, :], sim[0, 0, 0:rows, :]
     k = ones[0:rows, :] % 4
     re_ref[...] = jnp.where(k == 0, a, jnp.where(k == 1, b, jnp.where(k == 2, -a, -b)))
@@ -198,27 +202,25 @@
     state_spec = P(('inst', 'qx', 'qy'))
     vmem = pl.BlockSpec(memory_space=pltpu.VMEM)
     smem = pl.BlockSpec(memory_space=pltpu.SMEM)
+    hbm = pl.BlockSpec(memory_space=pl.ANY)
 
     def device_body(cost_loc, gamma_angles, beta_angles):
         local = cost_loc.shape[0]
         rows = local // LANES
         total_bits = int(math.log2(local * nqx * nqy))
         layers = gamma_angles.shape[0]
-        cost2 = cost_loc.reshape(rows, LANES)
-        table = pl.pallas_call(
-            functools.partial(exchange_kernel, half, nqy),
-            out_shape=jax.ShapeDtypeStruct((half, 8, LANES), F32),
-            in_specs=[vmem], out_specs=vmem,
-            scratch_shapes=[pltpu.VMEM((8, LANES), F32), pltpu.SemaphoreType.DMA((half,)), pltpu.SemaphoreType.DMA((half,))],
+        st = jax.ShapeDtypeStruct((rows, LANES), F32)
+        state = pltpu.VMEM((2, 4, LANES, LANES), F32)
+        weights = pltpu.VMEM((layers, 3, 2 * LANES, 2 * LANES), BF16)
+        energy, re, im = pl.pallas_call(
+            functools.partial(kernel, layers, total_bits, half, nqy),
+            out_shape=(jax.ShapeDtypeStruct((1,), F32), st, st),
+            in_specs=[smem, smem, hbm], out_specs=(smem, vmem, vmem),
+            scratch_shapes=[pltpu.VMEM((rows, LANES), F32), pltpu.VMEM((half, 8, LANES), F32), pltpu.VMEM((8, LANES), F32),
+                            state, state, state, weights, weights,
+                            pltpu.SemaphoreType.DMA, pltpu.SemaphoreType.DMA((half,)), pltpu.SemaphoreType.DMA((half,))],
             compiler_params=pltpu.CompilerParams(collective_id=0, has_side_effects=True),
-        )(cost2)
-        st = jax.ShapeDtypeStruct((rows, LANES), F32)
-        energy, re, im = pl.pallas_call(
-            functools.partial(simulate_kernel, layers, total_bits),
-            out_shape=(jax.ShapeDtypeStruct((8, LANES), F32), st, st),
-            in_specs=[smem, smem, vmem, vmem], out_specs=(vmem, vmem, vmem),
-            scratch_shapes=[pltpu.VMEM((2, 4, LANES, LANES), F32)] * 3,
-        )(gamma_angles, beta_angles, cost2, table)
-        return energy[0, 0:1], re.reshape(local), im.reshape(local)
+        )(gamma_angles, beta_angles, cost_loc.reshape(rows, LANES))
+        return energy, re.reshape(local), im.reshape(local)
 
     return jax.shard_map(device_body, mesh=mesh, in_specs=(state_spec, P(), P()), out_specs=(P('inst'), state_spec, state_spec), check_vma=False)

time: 24.7 us -> 25.4 us (1.028)
  Pallas kernels: 22.7 us -> 20.9 us
  between operations: 0.64 us -> 2.33 us
  local copies, waits for them, and re-layouts: 1.19 us -> 2 us
    unnamed x0 -> x4, local copies, waits for them, and re-layouts: none -> 2 us
    pallas_call x2 -> x1, Pallas kernels: 22.7 us -> 20.9 us  [device_body(): pl.pallas_call(functools.partial(kernel, layers, total_bits, half, nqy),...]
    slice x1 -> x0, local copies, waits for them, and re-layouts: 1.19 us -> none  [device_body(): return (energy[0, 0:1], re.reshape(local), im.reshape(local))]
where the time goes in v1:
time: 25.4 us; the launch traced here: 25.2 us
  Pallas kernels  20.9 us (82%)
  between operations  2.33 us (9%)
  local copies, waits for them, and re-layouts  2 us (8%)
    pallas_call x1, Pallas kernels, device_body(): pl.pallas_call(functools.partial(kernel, layers, total_bits, half, nqy),...  20.9 us
    unnamed x4, local copies, waits for them, and re-layouts  2 us

profile of v1, /device:TPU:97, one launch (start us, length us, event | category | flops | bytes accessed | tf_op | source)
XLA Modules:
  0.0 25.2 jit_solution(2062821611719274847)
XLA Ops:
  0.6 20.9 %shard_map.58 = (f32[1]{0:T(128)}, f32[64,128]{1,0:T(8,128)}, f32[64,128]{1,0:T(8,128)}) custom-call(f32[4]{0:T(128)} %gamma_ref.1, f32[4]{0:T(128)} %beta_ref.1, f32[64,128]{1,0:T(8,128)} %bitcast.3), custom_call_target="tpu_custom_call" | custom-call | tf_op jit(solution)/shard_map/pallas_call | solution.py:215
  22.1 0.0 copy-start
  22.1 1.4 %copy.10 = f32[8192]{0:T(1024)} copy(f32[8192]{0:T(1024)} %bitcast.5) | data formatting | bytes 65536
  23.4 0.0 copy-done
  23.4 0.6 %copy.11 = f32[8192]{0:T(1024)} copy(f32[8192]{0:T(1024)S(1)} %bitcast.4) | data formatting | bytes 65536
Async XLA Ops:
  22.1 1.4 %copy-start = (f32[64,128]{1,0:T(8,128)S(1)}, f32[64,128]{1,0:T(8,128)}, u32[]{:S(2)}) copy-start(f32[64,128]{1,0:T(8,128)} %get-tuple-element.8) | copy-start | bytes 98308

commit v2 on v1

--- a/solution.py
+++ b/solution.py
@@ -76,10 +76,14 @@
     return jnp.concatenate(blocks, axis=0)
 
 
-def kernel(layers, total_bits, half, nqy, gamma_ref, beta_ref, cost_hbm, energy_ref, re_ref, im_ref,
-           cost_ref, table_ref, packet, cst, sre, sim, wcat_ref, mcat_ref, load_sem, send_sem, recv_sem):
+def kernel(layers, total_bits, half, nqy, gamma_hbm, beta_hbm, cost_hbm, energy_ref, re_ref, im_ref,
+           cost_ref, table_ref, packet, cst, sre, sim, wcat_ref, mcat_ref, gamma_ref, beta_ref, load_sem, angle_sem, send_sem, recv_sem):
     load = pltpu.make_async_copy(cost_hbm, cost_ref, load_sem)
     load.start()
+    angle_loads = [pltpu.make_async_copy(gamma_hbm, gamma_ref, angle_sem.at[0]),
+                   pltpu.make_async_copy(beta_hbm, beta_ref, angle_sem.at[1])]
+    for angle_load in angle_loads:
+        angle_load.start()
     me_x, me_y = lax.axis_index('qx'), lax.axis_index('qy')
     barrier = pltpu.get_barrier_semaphore()
 
@@ -103,6 +107,8 @@
             device_id=partner(e), device_id_type=pl.DeviceIdType.MESH)
         copy.start()
         copies.append(copy)
+    for angle_load in angle_loads:
+        angle_load.wait()
     trig = []
     for l in range(layers):
         half_beta = jnp.full((8, LANES), 0.5, F32) * beta_ref[l]
@@ -189,11 +195,17 @@
         for u in range(4):
             a, b = sre[t, u], sim[t, u]
             total = total + cst[t, u] * (a * a + b * b)
-    energy_ref[0] = 2.0 * jnp.sum(total)
+    energy_ref[...] = jnp.sum(total.reshape(16, 8, LANES), axis=0)
     a, b = sre[0, 0, 0:rows, :], sim[0, 0, 0:rows, :]
     k = ones[0:rows, :] % 4
     re_ref[...] = jnp.where(k == 0, a, jnp.where(k == 1, b, jnp.where(k == 2, -a, -b)))
     im_ref[...] = jnp.where(k == 0, b, jnp.where(k == 1, -a, jnp.where(k == 2, -b, a)))
+
+
+def write_kernel(partial_ref, re_in, im_in, energy_ref, re_ref, im_ref):
+    re_ref[...] = re_in[...]
+    im_ref[...] = im_in[...]
+    energy_ref[0] = 2.0 * jnp.sum(partial_ref[...])
 
 
 def solution(mesh):
@@ -202,7 +214,7 @@
     state_spec = P(('inst', 'qx', 'qy'))
     vmem = pl.BlockSpec(memory_space=pltpu.VMEM)
     smem = pl.BlockSpec(memory_space=pltpu.SMEM)
-    hbm = pl.BlockSpec(memory_space=pl.ANY)
+    hbm = pl.BlockSpec(memory_space=pltpu.HBM)
 
     def device_body(cost_loc, gamma_angles, beta_angles):
         local = cost_loc.shape[0]
@@ -212,15 +224,22 @@
         st = jax.ShapeDtypeStruct((rows, LANES), F32)
         state = pltpu.VMEM((2, 4, LANES, LANES), F32)
         weights = pltpu.VMEM((layers, 3, 2 * LANES, 2 * LANES), BF16)
-        energy, re, im = pl.pallas_call(
+        partial, re, im = pl.pallas_call(
             functools.partial(kernel, layers, total_bits, half, nqy),
-            out_shape=(jax.ShapeDtypeStruct((1,), F32), st, st),
-            in_specs=[smem, smem, hbm], out_specs=(smem, vmem, vmem),
+            out_shape=(jax.ShapeDtypeStruct((8, LANES), F32), st, st),
+            in_specs=[hbm, hbm, hbm], out_specs=(vmem, vmem, vmem),
             scratch_shapes=[pltpu.VMEM((rows, LANES), F32), pltpu.VMEM((half, 8, LANES), F32), pltpu.VMEM((8, LANES), F32),
                             state, state, state, weights, weights,
-                            pltpu.SemaphoreType.DMA, pltpu.SemaphoreType.DMA((half,)), pltpu.SemaphoreType.DMA((half,))],
-            compiler_params=pltpu.CompilerParams(collective_id=0, has_side_effects=True),
-        )(gamma_angles, beta_angles, cost_loc.reshape(rows, LANES))
+                            pltpu.SMEM(gamma_angles.shape, F32), pltpu.SMEM(beta_angles.shape, F32),
+                            pltpu.SemaphoreType.DMA, pltpu.SemaphoreType.DMA((2,)),
+                            pltpu.SemaphoreType.DMA((half,)), pltpu.SemaphoreType.DMA((half,))],
+            compiler_params=pltpu.CompilerParams(collective_id=0, has_side_effects=True, vmem_limit_bytes=32 * 1024 * 1024),
+        )(*[pltpu.with_memory_space_constraint(x, pltpu.HBM) for x in (gamma_angles, beta_angles, cost_loc.reshape(rows, LANES))])
+        energy, re, im = pl.pallas_call(
+            write_kernel, out_shape=(jax.ShapeDtypeStruct((1,), F32), st, st),
+            in_specs=[vmem, vmem, vmem], out_specs=(smem, vmem, vmem),
+            compiler_params=pltpu.CompilerParams(vmem_limit_bytes=4 * 1024 * 1024),
+        )(partial, re, im)
         return energy, re.reshape(local), im.reshape(local)
 
     return jax.shard_map(device_body, mesh=mesh, in_specs=(state_spec, P(), P()), out_specs=(P('inst'), state_spec, state_spec), check_vma=False)

time: 25.4 us -> 21 us (0.83)
  local copies, waits for them, and re-layouts: 2 us -> 0 us
  between operations: 2.33 us -> 0.64 us
  Pallas kernels: 20.9 us -> 20.2 us
    unnamed x4 -> x0, local copies, waits for them, and re-layouts: 2 us -> none
    pallas_call x1, Pallas kernels: 20.9 us -> 19.6 us  [device_body(): pl.pallas_call(functools.partial(kernel, layers, total_bits, half, nqy),...]
    pallas_call x0 -> x1, Pallas kernels: none -> 0.64 us  [device_body(): pl.pallas_call(write_kernel, out_shape=(jax.ShapeDtypeStruct((1,), F32),...]
where the time goes in v2:
time: 21 us; the launch traced here: 20.9 us
  Pallas kernels  20.2 us (96%)
  between operations  0.64 us (3%)
    pallas_call x1, Pallas kernels, device_body(): pl.pallas_call(functools.partial(kernel, layers, total_bits, half, nqy),...  19.6 us
    pallas_call x1, Pallas kernels, device_body(): pl.pallas_call(write_kernel, out_shape=(jax.ShapeDtypeStruct((1,), F32),...  0.64 us

profile of v2, /device:TPU:97, one launch (start us, length us, event | category | flops | bytes accessed | tf_op | source)
XLA Modules:
  0.0 20.9 jit_solution(18417067749519187143)
XLA Ops:
  0.6 19.6 %shard_map.58 = (f32[8,128]{1,0:T(8,128)S(1)}, f32[64,128]{1,0:T(8,128)S(1)}, f32[64,128]{1,0:T(8,128)S(1)}) custom-call(f32[4]{0:T(128)} %gamma_hbm.1, f32[4]{0:T(128)} %beta_hbm.1, f32[64,128]{1,0:T(8,128)} %bitcast.3), custom_call_target="tpu_custom_call" | custom-call | tf_op jit(solution)/shard_map/pallas_call | solution.py:227
  20.2 0.6 %shard_map.59 = (f32[1]{0:T(128)}, f32[64,128]{1,0:T(8,128)}, f32[64,128]{1,0:T(8,128)}) custom-call(f32[8,128]{1,0:T(8,128)S(1)} %get-tuple-element.9.partial_ref, f32[64,128]{1,0:T(8,128)S(1)} %get-tuple-element.10.re_in, f32[64,128]{1,0:T(8,128)S(1)} %get-tuple-element.11.im_in), custom_call_target="tpu_custom_call" | custom-call | tf_op jit(solution)/shard_map/pallas_call | solution.py:238

commit v3 on v2

v3 whole, which is shorter than its diff:
```python
import functools
import math
import jax
import jax.numpy as jnp
from jax import lax
from jax.experimental import pallas as pl
from jax.experimental.pallas import tpu as pltpu
from jax.sharding import PartitionSpec as P

LANES = 128
SIN_POLY = (4.442883014678955, -7.308245658874512, 3.606354236602783, -0.8461116552352905, 0.1098245158791542)
COS_POLY = (1.4142135381698608, -6.9788641929626465, 5.73988151550293, -1.888274908065796, 0.33225154876708984, -0.034501612186431885)
F32 = jnp.float32
BF16 = jnp.bfloat16


def flip_bits(value, mask):
    bit = 1
    while bit <= mask:
        if mask & bit:
            value = value + bit * (1 - 2 * ((value // bit) % 2))
        bit *= 2
    return value


def turn_cos_sin(turns):
    rem = turns - jnp.round(turns)
    sq = rem * rem
    s = SIN_POLY[-1]
    for k in SIN_POLY[-2::-1]:
        s = s * sq + k
    s = s * rem
    c = COS_POLY[-1]
    for k in COS_POLY[-2::-1]:
        c = c * sq + k
    return 1.0 - s * s, s * c


def split3(x):
    a = x.astype(BF16)
    r = x - a.astype(F32)
    b = r.astype(BF16)
    c = (r - b.astype(F32)).astype(BF16)
    return a, b, c


def reverse_rows(x):
    n = x.shape[0]
    i = lax.broadcasted_iota(jnp.int32, (n, n), 0)
    j = lax.broadcasted_iota(jnp.int32, (n, n), 1)
    perm = jnp.where(i + j == n - 1, 1.0, 0.0).astype(F32)
    return jnp.dot(perm, x, precision=lax.Precision.HIGHEST, preferred_element_type=F32)


def product_matrix(diag, off0, off1, scale):
    lane = lax.broadcasted_iota(jnp.int32, (8, LANES), 1)
    sub = lax.broadcasted_iota(jnp.int32, (8, LANES), 0)
    bit = lambda v, b: (v // (1 << b)) % 2
    base = jnp.full((8, LANES), 1.0, F32) * scale
    rows = [[None, None] for _ in range(7)]
    for b in range(7):
        lb = bit(lane, b) == 1
        row0 = jnp.where(lb, off0, diag[0])
        row1 = jnp.where(lb, diag[1], off1)
        rows[b] = [row0, row1]
    for b in range(3):
        base = base * jnp.where(bit(sub, b) == 1, rows[b][1], rows[b][0])
    blocks = [base]
    for b in range(3, 7):
        blocks = [x * rows[b][0] for x in blocks] + [x * rows[b][1] for x in blocks]
    return jnp.concatenate(blocks, axis=0)


CHUNKS = 4


def kernel(layers, total_bits, half, nqy, gamma_hbm, beta_hbm, cost_hbm, energy_ref, re_ref, im_ref,
           cost_ref, table_ref, packet, cst, base_ref, start_ref, low_ref, high_ref, ph_ref, sx, lx, w_ref, h_ref, trig_ref, gamma_ref, beta_ref,
           load_sem, angle_sem, send_sem, recv_sem):
    load = pltpu.make_async_copy(cost_hbm, cost_ref, load_sem)
    load.start()
    angle_loads = [pltpu.make_async_copy(gamma_hbm, gamma_ref, angle_sem.at[0]),
                   pltpu.make_async_copy(beta_hbm, beta_ref, angle_sem.at[1])]
    for angle_load in angle_loads:
        angle_load.start()
    me_x, me_y = lax.axis_index('qx'), lax.axis_index('qy')
    barrier = pltpu.get_barrier_semaphore()
    partners = {e: {'qx': flip_bits(me_x, e // nqy), 'qy': flip_bits(me_y, e % nqy)} for e in range(1, half)}
    order = sorted(range(1, half), key=lambda e: (-(e // (2 * nqy)) - (0, 1, 2, 1)[e % nqy], e))
    for e in order:
        pl.semaphore_signal(barrier, inc=1, device_id=partners[e], device_id_type=pl.DeviceIdType.MESH)
    load.wait()
    rows = cost_ref.shape[0]
    row_bits = int(math.log2(rows))
    lane1 = lax.broadcasted_iota(jnp.int32, (1, LANES), 1)
    slopes = jnp.zeros((1, LANES), F32)
    for k in range(row_bits):
        row = cost_ref[(1 << k):(1 << k) + 1, :]
        slopes = jnp.where(lane1 == k, row if k == 0 else pltpu.roll(row, k, axis=1), slopes)
    packet[0:1, :] = cost_ref[0:1, :]
    packet[1:2, :] = slopes
    pl.semaphore_wait(barrier, half - 1)
    copies = {}
    for e in order:
        copies[e] = pltpu.make_async_remote_copy(
            src_ref=packet.at[0:2], dst_ref=table_ref.at[e, 0:2], send_sem=send_sem.at[e], recv_sem=recv_sem.at[e],
            device_id=partners[e], device_id_type=pl.DeviceIdType.MESH)
        copies[e].start()
    for angle_load in angle_loads:
        angle_load.wait()
    zero = jnp.zeros((LANES, LANES), BF16)
    for l in range(layers):
        half_beta = jnp.full((8, LANES), 0.5, F32) * beta_ref[l]
        c, s = jnp.cos(half_beta), jnp.sin(half_beta)
        a = product_matrix((c, c), -s, s, 0.5 * c)
        b = product_matrix((-s, -s), -c, c, -0.5 * s)
        a_t = product_matrix((c, c), s, -s, 0.25 * c)
        b_t = product_matrix((-s, -s), c, -c, -0.25 * s)
        for pq in range(2):
            g1, g2, g3 = split3(a - b if pq else a + b)
            w_ref[l, pq] = jnp.concatenate([jnp.concatenate([g1, g1, g1, zero], axis=1),
                                            jnp.concatenate([g2, g2, zero, g3], axis=1)], axis=0)
            h1, h2, h3 = split3(a_t - b_t if pq else a_t + b_t)
            h_ref[l, pq] = jnp.concatenate([jnp.concatenate([h1, h1, h1, zero], axis=0),
                                            jnp.concatenate([h2, h2, zero, h3], axis=0)], axis=1)
        trig_ref[l, 0] = c * c - s * s
        trig_ref[l, 1] = 2.0 * (s * c)

    lane = lax.broadcasted_iota(jnp.int32, (LANES, LANES), 1)
    vrow = lax.broadcasted_iota(jnp.int32, (LANES, LANES), 0)
    ones = jnp.zeros((LANES, LANES), jnp.int32)
    for b in range(7):
        ones = ones + (lane // (1 << b)) % 2 + (vrow // (1 << b)) % 2
    ones = ones % 4
    quarter = ones.astype(F32) * 0.25
    amp = 2.0 ** (-total_bits / 2.0)
    cost = cost_ref[...]
    bases = (cost, reverse_rows(cost))
    sub = lax.broadcasted_iota(jnp.int32, (8, LANES), 0)

    def unit(turns):
        co, si = turn_cos_sin(turns)
        return co, -si

    def mul(x, y):
        return x[0] * y[0] - x[1] * y[1], x[0] * y[1] + x[1] * y[0]

    rates = [gamma_ref[l] * (1.0 / (2.0 * math.pi)) for l in range(layers)]
    for t in range(2):
        for l in range(1, layers):
            for i, x in enumerate(unit(bases[t] * rates[l])):
                base_ref[l, t, i] = x
        turns = bases[t] * rates[0]
        turns = turns - jnp.round(turns) - quarter[:rows]
        re, im = unit(turns)
        re, im = amp * re, amp * im
        for e0s, pair in enumerate(((re, im), (-im, re))):
            for i, x in enumerate(pair):
                start_ref[t, e0s, i] = x

    def place(e):
        t = e // (2 * nqy)
        return t, e % nqy, (e // nqy) % 2 ^ t

    def put_state(u, lo, x0, x1):
        n = x0.shape[0]
        for pq, x in enumerate((x0 + x1, x0 - x1)):
            for k, part in enumerate(split3(x)):
                sx[u, pq, k, lo:lo + n, :] = part

    def rows_stage(l, u):
        out = []
        for pq in range(2):
            x = [sx[u, pq, k] for k in range(3)]
            y = jnp.dot(w_ref[l, pq], jnp.concatenate(x + x[:1], axis=0), preferred_element_type=F32)
            out.append(y[:LANES] + y[LANES:])
        return out

    def put_pair(u, ys):
        step = LANES // CHUNKS
        for a, b in ((u, 3 - u), (3 - u, u)):
            y0 = ys[a][0] + ys[a][1]
            y1 = ys[b][0] - ys[b][1]
            for pq, y in enumerate((y0 + y1, y0 - y1)):
                for k, part in enumerate(split3(y)):
                    for j in range(CHUNKS):
                        for i in range(2):
                            lo = (a * 2 + i) * step
                            lx[j, pq, k, lo:lo + step, :] = part[j * step:(j + 1) * step, i * LANES:(i + 1) * LANES]

    def lanes_stage(l, j):
        cb, sb = trig_ref[l, 0, 0:1, :], trig_ref[l, 1, 0:1, :]
        step = LANES // CHUNKS
        psi = []
        for pq in range(2):
            x = [lx[j, pq, k] for k in range(3)]
            z = jnp.dot(jnp.concatenate(x + x[:1], axis=1), h_ref[l, pq], preferred_element_type=F32)
            z = z[:, :LANES] + z[:, LANES:]
            f = [[z[(u * 2 + i) * step:(u * 2 + i + 1) * step] for i in range(2)] for u in range(4)]
            p = [f[0][i] + f[3][i] for i in range(2)]
            m = [f[0][i] - f[3][i] for i in range(2)]
            q = [f[1][i] + f[2][i] for i in range(2)]
            n = [f[1][i] - f[2][i] for i in range(2)]
            p, q = ((cb * p[0] + sb * q[1], cb * p[1] - sb * q[0]), (cb * q[0] + sb * p[1], cb * q[1] - sb * p[0]))
            psi.append([[p[i] + m[i] for i in range(2)], [q[i] + n[i] for i in range(2)],
                        [q[i] - n[i] for i in range(2)], [p[i] - m[i] for i in range(2)]])
        first = [[psi[0][u][i] + psi[1][u][i] for i in range(2)] for u in range(4)]
        second = [[psi[0][3 - u][i] - psi[1][3 - u][i] for i in range(2)] for u in range(4)]
        return first, second

    for e in order:
        copies[e].wait()
    first = jnp.concatenate([(table_ref[e, 0:1, :] - cost[0:1, :]) if e else jnp.zeros((1, LANES), F32) for e in range(half)], axis=0)
    slope = jnp.concatenate([(table_ref[e, 1:2, :] - slopes) if e else jnp.zeros((1, LANES), F32) for e in range(half)], axis=0)
    slope = slope - first[:, 0:1]
    cols = [jnp.broadcast_to(slope[:, k:k + 1], (half, LANES)) for k in range(row_bits)]
    low = {}
    for e in range(1, half):
        part = jnp.broadcast_to(first[e:e + 1, :], (8, LANES))
        for k in range(3):
            part = part + jnp.where((sub // (1 << k)) % 2 == 1 - e // (2 * nqy), cols[k][e:e + 1, :], 0.0)
        low[e] = part

    def put_factors(l):
        for k in range(3, row_bits):
            for i, x in enumerate(unit(cols[k] * rates[l])):
                high_ref[l, k - 3, i] = x
        for e in range(1, half):
            for i, x in enumerate(unit(low[e] * rates[l])):
                low_ref[l, e, i] = x

    def factors(l, e):
        out = [(low_ref[l, e, 0], low_ref[l, e, 1])]
        for k in range(row_bits - 3):
            h = (high_ref[l, k, 0, e:e + 1, :], high_ref[l, k, 1, e:e + 1, :])
            more = [mul(x, h) for x in out]
            out = more + out if e // (2 * nqy) else out + more
        return [jnp.concatenate([x[i] for x in out], axis=0) for i in range(2)]

    def put_phases(l, us):
        for e in range(half):
            t, u, e0s = place(e)
            if u in us:
                x = (base_ref[l, t, 0], base_ref[l, t, 1])
                if e:
                    x = mul(x, factors(l, e))
                for i in range(2):
                    ph_ref[t, u, i, e0s * rows:(e0s + 1) * rows, :] = x[i]

    def put_cost(us):
        for e in range(half):
            t, u, e0s = place(e)
            if u in us:
                block = bases[t]
                if e:
                    parts = [low[e]]
                    for k in range(3, row_bits):
                        more = [x + cols[k][e:e + 1, :] for x in parts]
                        parts = more + parts if t else parts + more
                    block = block + jnp.concatenate(parts, axis=0)
                cst[t, u, e0s * rows:(e0s + 1) * rows, :] = block

    put_factors(0)
    ys = {}
    for u in (0, 3, 1, 2):
        xs = [[None, None], [None, None]]
        for e in range(half):
            if e % nqy == u:
                t, _, e0s = place(e)
                x = (start_ref[t, e0s, 0], start_ref[t, e0s, 1])
                xs[t][e0s] = jnp.concatenate(mul(x, factors(0, e)) if e else x, axis=1)
        put_state(u, 0, *[jnp.concatenate(x, axis=0) for x in xs])
        ys[u] = rows_stage(0, u)
        if u == 3:
            put_pair(0, ys)
        if u == 2:
            put_pair(1, ys)
    put_factors(1)
    put_phases(1, range(nqy))

    step = LANES // CHUNKS
    total = jnp.zeros((8, LANES), F32)
    for l in range(layers):
        for j in range(CHUNKS):
            both = lanes_stage(l, j)
            at = pl.ds(j * step, step)
            if l < layers - 1:
                for u in range(4):
                    xs = []
                    for t in range(2):
                        a, b = both[t][u]
                        pr, pi = ph_ref[t, u, 0, at, :], ph_ref[t, u, 1, at, :]
                        xs.append(jnp.concatenate([a * pr - b * pi, b * pr + a * pi], axis=1))
                    put_state(u, j * step, *xs)
            else:
                for u in range(4):
                    for t in range(2):
                        a, b = both[t][u]
                        total = total + jnp.sum((cst[t, u, at, :] * (a * a + b * b)).reshape(step // 8, 8, LANES), axis=0)
                if j * step < rows:
                    a, b = both[0][0]
                    k = ones[j * step:(j + 1) * step, :]
                    re_ref[at, :] = jnp.where(k == 0, a, jnp.where(k == 1, b, jnp.where(k == 2, -a, -b)))
                    im_ref[at, :] = jnp.where(k == 0, b, jnp.where(k == 1, -a, jnp.where(k == 2, -b, a)))
        if l < layers - 1:
            ys = {}
            for u in (0, 3, 1, 2):
                ys[u] = rows_stage(l + 1, u)
                if u == 3:
                    put_pair(0, ys)
                if u == 2:
                    put_pair(1, ys)
            if l + 2 < layers:
                put_factors(l + 2)
                put_phases(l + 2, range(nqy))
            else:
                put_cost(range(nqy))
    energy_ref[...] = total


def write_kernel(partial_ref, re_in, im_in, energy_ref, re_ref, im_ref):
    re_ref[...] = re_in[...]
    im_ref[...] = im_in[...]
    energy_ref[0] = 2.0 * jnp.sum(partial_ref[...])


def solution(mesh):
    nqx, nqy = mesh.shape['qx'], mesh.shape['qy']
    half = nqx * nqy // 2
    state_spec = P(('inst', 'qx', 'qy'))
    vmem = pl.BlockSpec(memory_space=pltpu.VMEM)
    smem = pl.BlockSpec(memory_space=pltpu.SMEM)
    hbm = pl.BlockSpec(memory_space=pltpu.HBM)

    def device_body(cost_loc, gamma_angles, beta_angles):
        local = cost_loc.shape[0]
        rows = local // LANES
        total_bits = int(math.log2(local * nqx * nqy))
        layers = gamma_angles.shape[0]
        st = jax.ShapeDtypeStruct((rows, LANES), F32)
        partial, re, im = pl.pallas_call(
            functools.partial(kernel, layers, total_bits, half, nqy),
            out_shape=(jax.ShapeDtypeStruct((8, LANES), F32), st, st),
            in_specs=[hbm, hbm, hbm], out_specs=(vmem, vmem, vmem),
            scratch_shapes=[pltpu.VMEM((rows, LANES), F32), pltpu.VMEM((half, 8, LANES), F32), pltpu.VMEM((8, LANES), F32),
                            pltpu.VMEM((2, 4, LANES, LANES), F32),
                            pltpu.VMEM((layers, 2, 2, rows, LANES), F32), pltpu.VMEM((2, 2, 2, rows, LANES), F32),
                            pltpu.VMEM((layers, half, 2, 8, LANES), F32), pltpu.VMEM((layers, 3, 2, half, LANES), F32),
                            pltpu.VMEM((2, 4, 2, LANES, LANES), F32),
                            pltpu.VMEM((4, 2, 3, LANES, 2 * LANES), BF16), pltpu.VMEM((CHUNKS, 2, 3, 8 * LANES // CHUNKS, LANES), BF16),
                            pltpu.VMEM((layers, 2, 2 * LANES, 4 * LANES), BF16), pltpu.VMEM((layers, 2, 4 * LANES, 2 * LANES), BF16),
                            pltpu.VMEM((layers, 2, 8, LANES), F32),
                            pltpu.SMEM(gamma_angles.shape, F32), pltpu.SMEM(beta_angles.shape, F32),
                            pltpu.SemaphoreType.DMA, pltpu.SemaphoreType.DMA((2,)),
                            pltpu.SemaphoreType.DMA((half,)), pltpu.SemaphoreType.DMA((half,))],
            compiler_params=pltpu.CompilerParams(collective_id=0, has_side_effects=True, vmem_limit_bytes=32 * 1024 * 1024),
        )(*[pltpu.with_memory_space_constraint(x, pltpu.HBM) for x in (gamma_angles, beta_angles, cost_loc.reshape(rows, LANES))])
        energy, re, im = pl.pallas_call(
            write_kernel, out_shape=(jax.ShapeDtypeStruct((1,), F32), st, st),
            in_specs=[vmem, vmem, vmem], out_specs=(smem, vmem, vmem),
            compiler_params=pltpu.CompilerParams(vmem_limit_bytes=4 * 1024 * 1024),
        )(partial, re, im)
        return energy, re.reshape(local), im.reshape(local)

    return jax.shard_map(device_body, mesh=mesh, in_specs=(state_spec, P(), P()), out_specs=(P('inst'), state_spec, state_spec), check_vma=False)
```

time: 21 us -> 18.4 us (0.88)
  Pallas kernels: 20.2 us -> 17.6 us
    pallas_call x1, Pallas kernels: 19.6 us -> 16.9 us  [device_body(): pl.pallas_call(functools.partial(kernel, layers, total_bits, half, nqy),...]
where the time goes in v3:
time: 18.4 us; the launch traced here: 18.2 us
  Pallas kernels  17.6 us (96%)
  between operations  0.64 us (3%)
    pallas_call x1, Pallas kernels, device_body(): pl.pallas_call(functools.partial(kernel, layers, total_bits, half, nqy),...  16.9 us
    pallas_call x1, Pallas kernels, device_body(): pl.pallas_call(write_kernel, out_shape=(jax.ShapeDtypeStruct((1,), F32),...  0.64 us

profile of v3, /device:TPU:97, one launch (start us, length us, event | category | flops | bytes accessed | tf_op | source)
XLA Modules:
  0.0 18.2 jit_solution(12798388925786685268)
XLA Ops:
  0.6 16.9 %shard_map.58 = (f32[8,128]{1,0:T(8,128)S(1)}, f32[64,128]{1,0:T(8,128)S(1)}, f32[64,128]{1,0:T(8,128)S(1)}) custom-call(f32[4]{0:T(128)} %gamma_hbm.1, f32[4]{0:T(128)} %beta_hbm.1, f32[64,128]{1,0:T(8,128)} %bitcast.3), custom_call_target="tpu_custom_call" | custom-call | tf_op jit(solution)/shard_map/pallas_call | solution.py:341
  17.6 0.6 %shard_map.59 = (f32[1]{0:T(128)}, f32[64,128]{1,0:T(8,128)}, f32[64,128]{1,0:T(8,128)}) custom-call(f32[8,128]{1,0:T(8,128)S(1)} %get-tuple-element.9.partial_ref, f32[64,128]{1,0:T(8,128)S(1)} %get-tuple-element.10.re_in, f32[64,128]{1,0:T(8,128)S(1)} %get-tuple-element.11.im_in), custom_call_target="tpu_custom_call" | custom-call | tf_op jit(solution)/shard_map/pallas_call | solution.py:358

commit v4 on v3

--- a/solution.py
+++ b/solution.py
@@ -8,6 +8,7 @@
 from jax.sharding import PartitionSpec as P
 
 LANES = 128
+QUAD = 4
 SIN_POLY = (4.442883014678955, -7.308245658874512, 3.606354236602783, -0.8461116552352905, 0.1098245158791542)
 COS_POLY = (1.4142135381698608, -6.9788641929626465, 5.73988151550293, -1.888274908065796, 0.33225154876708984, -0.034501612186431885)
 F32 = jnp.float32
@@ -42,6 +43,19 @@
     b = r.astype(BF16)
     c = (r - b.astype(F32)).astype(BF16)
     return a, b, c
+
+
+def missing(diff, e):
+    bits = [1 << b for b in range(e.bit_length()) if e >> b & 1]
+    if len(bits) == 2:
+        a, b = bits
+        c = next(1 << k for k in range(4) if not e >> k & 1 and all(x in diff for x in (e | 1 << k, a | 1 << k, b | 1 << k)))
+        return diff[e | c] - diff[a | c] - diff[b | c] + diff[a] + diff[b] + diff[c]
+    pairs = [a | b for i, a in enumerate(bits) for b in bits[:i]]
+    total = diff[pairs[0]]
+    for p in pairs[1:]:
+        total = total + diff[p]
+    return total - (len(bits) - 2.0) * sum((diff[b] for b in bits[1:]), diff[bits[0]])
 
 
 def reverse_rows(x):
@@ -71,11 +85,11 @@
     return jnp.concatenate(blocks, axis=0)
 
 
-CHUNKS = 4
+CHUNKS = ((0, 32), (32, 32), (64, 32), (96, 32))
 
 
 def kernel(layers, total_bits, half, nqy, gamma_hbm, beta_hbm, cost_hbm, energy_ref, re_ref, im_ref,
-           cost_ref, table_ref, packet, cst, base_ref, start_ref, low_ref, high_ref, ph_ref, sx, lx, w_ref, h_ref, trig_ref, gamma_ref, beta_ref,
+           cost_ref, table_ref, diff_ref, packet, cst, base_ref, start_ref, low_ref, high_ref, ph_ref, sx, lx, w_ref, h_ref, trig_ref, gamma_ref, beta_ref,
            load_sem, angle_sem, send_sem, recv_sem):
     load = pltpu.make_async_copy(cost_hbm, cost_ref, load_sem)
     load.start()
@@ -85,8 +99,11 @@
         angle_load.start()
     me_x, me_y = lax.axis_index('qx'), lax.axis_index('qy')
     barrier = pltpu.get_barrier_semaphore()
-    partners = {e: {'qx': flip_bits(me_x, e // nqy), 'qy': flip_bits(me_y, e % nqy)} for e in range(1, half)}
-    order = sorted(range(1, half), key=lambda e: (-(e // (2 * nqy)) - (0, 1, 2, 1)[e % nqy], e))
+    near = nqy // 2
+    hops = {e: (0, 1, 2, 1)[e // (2 * near)] + e % near for e in range(1, half)}
+    asked = [e for e in hops if hops[e] < 2 or (hops[e] == 2 and (e // near) % 2 == 0)]
+    order = sorted(asked, key=lambda e: (-hops[e], e))
+    partners = {e: {'qx': flip_bits(me_x, e // near), 'qy': flip_bits(me_y, e % near)} for e in order}
     for e in order:
         pl.semaphore_signal(barrier, inc=1, device_id=partners[e], device_id_type=pl.DeviceIdType.MESH)
     load.wait()
@@ -99,11 +116,12 @@
         slopes = jnp.where(lane1 == k, row if k == 0 else pltpu.roll(row, k, axis=1), slopes)
     packet[0:1, :] = cost_ref[0:1, :]
     packet[1:2, :] = slopes
-    pl.semaphore_wait(barrier, half - 1)
+    own = packet[...]
+    pl.semaphore_wait(barrier, len(order))
     copies = {}
     for e in order:
         copies[e] = pltpu.make_async_remote_copy(
-            src_ref=packet.at[0:2], dst_ref=table_ref.at[e, 0:2], send_sem=send_sem.at[e], recv_sem=recv_sem.at[e],
+            src_ref=packet, dst_ref=table_ref.at[:, e], send_sem=send_sem.at[e], recv_sem=recv_sem.at[e],
             device_id=partners[e], device_id_type=pl.DeviceIdType.MESH)
         copies[e].start()
     for angle_load in angle_loads:
@@ -159,8 +177,8 @@
                 start_ref[t, e0s, i] = x
 
     def place(e):
-        t = e // (2 * nqy)
-        return t, e % nqy, (e // nqy) % 2 ^ t
+        t = e // (2 * QUAD)
+        return t, e % QUAD, (e // QUAD) % 2 ^ t
 
     def put_state(u, lo, x0, x1):
         n = x0.shape[0]
@@ -177,30 +195,32 @@
         return out
 
     def put_pair(u, ys):
-        step = LANES // CHUNKS
         for a, b in ((u, 3 - u), (3 - u, u)):
             y0 = ys[a][0] + ys[a][1]
             y1 = ys[b][0] - ys[b][1]
             for pq, y in enumerate((y0 + y1, y0 - y1)):
                 for k, part in enumerate(split3(y)):
-                    for j in range(CHUNKS):
-                        for i in range(2):
-                            lo = (a * 2 + i) * step
-                            lx[j, pq, k, lo:lo + step, :] = part[j * step:(j + 1) * step, i * LANES:(i + 1) * LANES]
-
-    def lanes_stage(l, j):
+                    for i in range(2):
+                        lx[pq, k, a, i] = part[:, i * LANES:(i + 1) * LANES]
+
+    def lanes_dot(l, pair, lo, n):
+        out = {}
+        for pq in range(2):
+            x = [jnp.concatenate([lx[pq, k, u, i, lo:lo + n, :] for u in pair for i in range(2)], axis=0) for k in range(3)]
+            z = jnp.dot(jnp.concatenate(x + x[:1], axis=1), h_ref[l, pq], preferred_element_type=F32)
+            z = z[:, :LANES] + z[:, LANES:]
+            for a, u in enumerate(pair):
+                out[pq, u] = [z[(a * 2 + i) * n:(a * 2 + i + 1) * n] for i in range(2)]
+        return out
+
+    def mix_pairs(l, f):
         cb, sb = trig_ref[l, 0, 0:1, :], trig_ref[l, 1, 0:1, :]
-        step = LANES // CHUNKS
         psi = []
         for pq in range(2):
-            x = [lx[j, pq, k] for k in range(3)]
-            z = jnp.dot(jnp.concatenate(x + x[:1], axis=1), h_ref[l, pq], preferred_element_type=F32)
-            z = z[:, :LANES] + z[:, LANES:]
-            f = [[z[(u * 2 + i) * step:(u * 2 + i + 1) * step] for i in range(2)] for u in range(4)]
-            p = [f[0][i] + f[3][i] for i in range(2)]
-            m = [f[0][i] - f[3][i] for i in range(2)]
-            q = [f[1][i] + f[2][i] for i in range(2)]
-            n = [f[1][i] - f[2][i] for i in range(2)]
+            p = [f[pq, 0][i] + f[pq, 3][i] for i in range(2)]
+            m = [f[pq, 0][i] - f[pq, 3][i] for i in range(2)]
+            q = [f[pq, 1][i] + f[pq, 2][i] for i in range(2)]
+            n = [f[pq, 1][i] - f[pq, 2][i] for i in range(2)]
             p, q = ((cb * p[0] + sb * q[1], cb * p[1] - sb * q[0]), (cb * q[0] + sb * p[1], cb * q[1] - sb * p[0]))
             psi.append([[p[i] + m[i] for i in range(2)], [q[i] + n[i] for i in range(2)],
                         [q[i] - n[i] for i in range(2)], [p[i] - m[i] for i in range(2)]])
@@ -208,17 +228,33 @@
         second = [[psi[0][3 - u][i] - psi[1][3 - u][i] for i in range(2)] for u in range(4)]
         return first, second
 
+    def lanes_stage(l):
+        half_rows = LANES // 2
+        early = [lanes_dot(l, (0, 3), lo, half_rows) for lo in (0, half_rows)]
+        for lo, n in CHUNKS:
+            f = lanes_dot(l, (1, 2), lo, n)
+            at = lo % half_rows
+            for key, x in early[lo // half_rows].items():
+                f[key] = [y[at:at + n] for y in x]
+            yield lo, n, mix_pairs(l, f)
+
     for e in order:
         copies[e].wait()
-    first = jnp.concatenate([(table_ref[e, 0:1, :] - cost[0:1, :]) if e else jnp.zeros((1, LANES), F32) for e in range(half)], axis=0)
-    slope = jnp.concatenate([(table_ref[e, 1:2, :] - slopes) if e else jnp.zeros((1, LANES), F32) for e in range(half)], axis=0)
-    slope = slope - first[:, 0:1]
-    cols = [jnp.broadcast_to(slope[:, k:k + 1], (half, LANES)) for k in range(row_bits)]
+    diff = {0: jnp.zeros((2, LANES), F32)}
+    for e in order:
+        diff[e] = table_ref[:, e] - own
+    for e in sorted(range(half), key=lambda e: bin(e).count('1')):
+        if e not in diff:
+            diff[e] = missing(diff, e)
+        diff_ref[:, e] = diff[e]
+    first = diff_ref[0]
+    corner = jnp.broadcast_to(diff_ref[0, :, 0:1], (half, LANES))
+    cols = [jnp.broadcast_to(diff_ref[1, :, k:k + 1], (half, LANES)) - corner for k in range(row_bits)]
     low = {}
     for e in range(1, half):
         part = jnp.broadcast_to(first[e:e + 1, :], (8, LANES))
         for k in range(3):
-            part = part + jnp.where((sub // (1 << k)) % 2 == 1 - e // (2 * nqy), cols[k][e:e + 1, :], 0.0)
+            part = part + jnp.where((sub // (1 << k)) % 2 == 1 - e // (2 * QUAD), cols[k][e:e + 1, :], 0.0)
         low[e] = part
 
     def put_factors(l):
@@ -234,7 +270,7 @@
         for k in range(row_bits - 3):
             h = (high_ref[l, k, 0, e:e + 1, :], high_ref[l, k, 1, e:e + 1, :])
             more = [mul(x, h) for x in out]
-            out = more + out if e // (2 * nqy) else out + more
+            out = more + out if e // (2 * QUAD) else out + more
         return [jnp.concatenate([x[i] for x in out], axis=0) for i in range(2)]
 
     def put_phases(l, us):
@@ -265,7 +301,7 @@
     for u in (0, 3, 1, 2):
         xs = [[None, None], [None, None]]
         for e in range(half):
-            if e % nqy == u:
+            if e % QUAD == u:
                 t, _, e0s = place(e)
                 x = (start_ref[t, e0s, 0], start_ref[t, e0s, 1])
                 xs[t][e0s] = jnp.concatenate(mul(x, factors(0, e)) if e else x, axis=1)
@@ -276,14 +312,12 @@
         if u == 2:
             put_pair(1, ys)
     put_factors(1)
-    put_phases(1, range(nqy))
-
-    step = LANES // CHUNKS
+    put_phases(1, range(QUAD))
+
     total = jnp.zeros((8, LANES), F32)
     for l in range(layers):
-        for j in range(CHUNKS):
-            both = lanes_stage(l, j)
-            at = pl.ds(j * step, step)
+        for lo, n, both in lanes_stage(l):
+            at = pl.ds(lo, n)
             if l < layers - 1:
                 for u in range(4):
                     xs = []
@@ -291,15 +325,15 @@
                         a, b = both[t][u]
                         pr, pi = ph_ref[t, u, 0, at, :], ph_ref[t, u, 1, at, :]
                         xs.append(jnp.concatenate([a * pr - b * pi, b * pr + a * pi], axis=1))
-                    put_state(u, j * step, *xs)
+                    put_state(u, lo, *xs)
             else:
                 for u in range(4):
                     for t in range(2):
                         a, b = both[t][u]
-                        total = total + jnp.sum((cst[t, u, at, :] * (a * a + b * b)).reshape(step // 8, 8, LANES), axis=0)
-                if j * step < rows:
+                        total = total + jnp.sum((cst[t, u, at, :] * (a * a + b * b)).reshape(n // 8, 8, LANES), axis=0)
+                if lo < rows:
                     a, b = both[0][0]
-                    k = ones[j * step:(j + 1) * step, :]
+                    k = ones[lo:lo + n, :]
                     re_ref[at, :] = jnp.where(k == 0, a, jnp.where(k == 1, b, jnp.where(k == 2, -a, -b)))
                     im_ref[at, :] = jnp.where(k == 0, b, jnp.where(k == 1, -a, jnp.where(k == 2, -b, a)))
         if l < layers - 1:
@@ -312,9 +346,9 @@
                     put_pair(1, ys)
             if l + 2 < layers:
                 put_factors(l + 2)
-                put_phases(l + 2, range(nqy))
+                put_phases(l + 2, range(QUAD))
             else:
-                put_cost(range(nqy))
+                put_cost(range(QUAD))
     energy_ref[...] = total
 
 
@@ -342,12 +376,12 @@
             functools.partial(kernel, layers, total_bits, half, nqy),
             out_shape=(jax.ShapeDtypeStruct((8, LANES), F32), st, st),
             in_specs=[hbm, hbm, hbm], out_specs=(vmem, vmem, vmem),
-            scratch_shapes=[pltpu.VMEM((rows, LANES), F32), pltpu.VMEM((half, 8, LANES), F32), pltpu.VMEM((8, LANES), F32),
+            scratch_shapes=[pltpu.VMEM((rows, LANES), F32), pltpu.VMEM((2, half, LANES), F32), pltpu.VMEM((2, half, LANES), F32), pltpu.VMEM((2, LANES), F32),
                             pltpu.VMEM((2, 4, LANES, LANES), F32),
                             pltpu.VMEM((layers, 2, 2, rows, LANES), F32), pltpu.VMEM((2, 2, 2, rows, LANES), F32),
                             pltpu.VMEM((layers, half, 2, 8, LANES), F32), pltpu.VMEM((layers, 3, 2, half, LANES), F32),
                             pltpu.VMEM((2, 4, 2, LANES, LANES), F32),
-                            pltpu.VMEM((4, 2, 3, LANES, 2 * LANES), BF16), pltpu.VMEM((CHUNKS, 2, 3, 8 * LANES // CHUNKS, LANES), BF16),
+                            pltpu.VMEM((4, 2, 3, LANES, 2 * LANES), BF16), pltpu.VMEM((2, 3, 4, 2, LANES, LANES), BF16),
                             pltpu.VMEM((layers, 2, 2 * LANES, 4 * LANES), BF16), pltpu.VMEM((layers, 2, 4 * LANES, 2 * LANES), BF16),
                             pltpu.VMEM((layers, 2, 8, LANES), F32),
                             pltpu.SMEM(gamma_angles.shape, F32), pltpu.SMEM(beta_angles.shape, F32),

time: 18.4 us -> 16.3 us (0.89)
  Pallas kernels: 17.6 us -> 15.5 us
    pallas_call x1, Pallas kernels: 16.9 us -> 14.8 us  [device_body(): pl.pallas_call(functools.partial(kernel, layers, total_bits, half, nqy),...]
where the time goes in v4:
time: 16.3 us; the launch traced here: 16.1 us
  Pallas kernels  15.5 us (95%)
  between operations  0.64 us (4%)
    pallas_call x1, Pallas kernels, device_body(): pl.pallas_call(functools.partial(kernel, layers, total_bits, half, nqy),...  14.8 us
    pallas_call x1, Pallas kernels, device_body(): pl.pallas_call(write_kernel, out_shape=(jax.ShapeDtypeStruct((1,), F32),...  0.64 us

profile of v4, /device:TPU:97, one launch (start us, length us, event | category | flops | bytes accessed | tf_op | source)
XLA Modules:
  0.0 16.1 jit_solution(16621743838112512303)
XLA Ops:
  0.6 14.8 %shard_map.58 = (f32[8,128]{1,0:T(8,128)S(1)}, f32[64,128]{1,0:T(8,128)S(1)}, f32[64,128]{1,0:T(8,128)S(1)}) custom-call(f32[4]{0:T(128)} %gamma_hbm.1, f32[4]{0:T(128)} %beta_hbm.1, f32[64,128]{1,0:T(8,128)} %bitcast.3), custom_call_target="tpu_custom_call" | custom-call | tf_op jit(solution)/shard_map/pallas_call | solution.py:375
  15.5 0.6 %shard_map.59 = (f32[1]{0:T(128)}, f32[64,128]{1,0:T(8,128)}, f32[64,128]{1,0:T(8,128)}) custom-call(f32[8,128]{1,0:T(8,128)S(1)} %get-tuple-element.9.partial_ref, f32[64,128]{1,0:T(8,128)S(1)} %get-tuple-element.10.re_in, f32[64,128]{1,0:T(8,128)S(1)} %get-tuple-element.11.im_in), custom_call_target="tpu_custom_call" | custom-call | tf_op jit(solution)/shard_map/pallas_call | solution.py:392

commit v5 on v4

--- a/solution.py
+++ b/solution.py
@@ -85,7 +85,8 @@
     return jnp.concatenate(blocks, axis=0)
 
 
-CHUNKS = ((0, 32), (32, 32), (64, 32), (96, 32))
+CHUNKS = ((0, 64, ((0, 64),)), (64, 64, ((64, 32), (96, 32))))
+LAST_CHUNKS = ((0, 64, ((0, 64),)), (64, 64, ((64, 48), (112, 16))))
 
 
 def kernel(layers, total_bits, half, nqy, gamma_hbm, beta_hbm, cost_hbm, energy_ref, re_ref, im_ref,
@@ -121,7 +122,7 @@
     copies = {}
     for e in order:
         copies[e] = pltpu.make_async_remote_copy(
-            src_ref=packet, dst_ref=table_ref.at[:, e], send_sem=send_sem.at[e], recv_sem=recv_sem.at[e],
+            src_ref=packet, dst_ref=table_ref.at[e], send_sem=send_sem.at[e], recv_sem=recv_sem.at[e],
             device_id=partners[e], device_id_type=pl.DeviceIdType.MESH)
         copies[e].start()
     for angle_load in angle_loads:
@@ -130,8 +131,8 @@
     for l in range(layers):
         half_beta = jnp.full((8, LANES), 0.5, F32) * beta_ref[l]
         c, s = jnp.cos(half_beta), jnp.sin(half_beta)
-        a = product_matrix((c, c), -s, s, 0.5 * c)
-        b = product_matrix((-s, -s), -c, c, -0.5 * s)
+        a = product_matrix((c, c), -s, s, c)
+        b = product_matrix((-s, -s), -c, c, -s)
         a_t = product_matrix((c, c), s, -s, 0.25 * c)
         b_t = product_matrix((-s, -s), c, -c, -0.25 * s)
         for pq in range(2):
@@ -195,13 +196,11 @@
         return out
 
     def put_pair(u, ys):
-        for a, b in ((u, 3 - u), (3 - u, u)):
-            y0 = ys[a][0] + ys[a][1]
-            y1 = ys[b][0] - ys[b][1]
-            for pq, y in enumerate((y0 + y1, y0 - y1)):
-                for k, part in enumerate(split3(y)):
-                    for i in range(2):
-                        lx[pq, k, a, i] = part[:, i * LANES:(i + 1) * LANES]
+        (p0, q0), (p3, q3) = ys[u], ys[3 - u]
+        for pq, v, y in ((0, u, p0 + p3), (0, 3 - u, q0 - q3), (1, u, q0 + q3), (1, 3 - u, p0 - p3)):
+            for k, part in enumerate(split3(y)):
+                for i in range(2):
+                    lx[pq, k, v, i] = part[:, i * LANES:(i + 1) * LANES]
 
     def lanes_dot(l, pair, lo, n):
         out = {}
@@ -217,10 +216,7 @@
         cb, sb = trig_ref[l, 0, 0:1, :], trig_ref[l, 1, 0:1, :]
         psi = []
         for pq in range(2):
-            p = [f[pq, 0][i] + f[pq, 3][i] for i in range(2)]
-            m = [f[pq, 0][i] - f[pq, 3][i] for i in range(2)]
-            q = [f[pq, 1][i] + f[pq, 2][i] for i in range(2)]
-            n = [f[pq, 1][i] - f[pq, 2][i] for i in range(2)]
+            p, q, n, m = [f[pq, u] for u in range(4)]
             p, q = ((cb * p[0] + sb * q[1], cb * p[1] - sb * q[0]), (cb * q[0] + sb * p[1], cb * q[1] - sb * p[0]))
             psi.append([[p[i] + m[i] for i in range(2)], [q[i] + n[i] for i in range(2)],
                         [q[i] - n[i] for i in range(2)], [p[i] - m[i] for i in range(2)]])
@@ -229,20 +225,19 @@
         return first, second
 
     def lanes_stage(l):
-        half_rows = LANES // 2
-        early = [lanes_dot(l, (0, 3), lo, half_rows) for lo in (0, half_rows)]
-        for lo, n in CHUNKS:
-            f = lanes_dot(l, (1, 2), lo, n)
-            at = lo % half_rows
-            for key, x in early[lo // half_rows].items():
-                f[key] = [y[at:at + n] for y in x]
-            yield lo, n, mix_pairs(l, f)
+        for start, size, chunks in CHUNKS if l < layers - 1 else LAST_CHUNKS:
+            early = lanes_dot(l, (0, 3), start, size)
+            for lo, n in chunks:
+                f = lanes_dot(l, (1, 2), lo, n)
+                for key, x in early.items():
+                    f[key] = [y[lo - start:lo - start + n] for y in x]
+                yield lo, n, mix_pairs(l, f)
 
     for e in order:
         copies[e].wait()
     diff = {0: jnp.zeros((2, LANES), F32)}
     for e in order:
-        diff[e] = table_ref[:, e] - own
+        diff[e] = table_ref[e] - own
     for e in sorted(range(half), key=lambda e: bin(e).count('1')):
         if e not in diff:
             diff[e] = missing(diff, e)
@@ -376,7 +371,7 @@
             functools.partial(kernel, layers, total_bits, half, nqy),
             out_shape=(jax.ShapeDtypeStruct((8, LANES), F32), st, st),
             in_specs=[hbm, hbm, hbm], out_specs=(vmem, vmem, vmem),
-            scratch_shapes=[pltpu.VMEM((rows, LANES), F32), pltpu.VMEM((2, half, LANES), F32), pltpu.VMEM((2, half, LANES), F32), pltpu.VMEM((2, LANES), F32),
+            scratch_shapes=[pltpu.VMEM((rows, LANES), F32), pltpu.VMEM((half, 2, LANES), F32), pltpu.VMEM((2, half, LANES), F32), pltpu.VMEM((2, LANES), F32),
                             pltpu.VMEM((2, 4, LANES, LANES), F32),
                             pltpu.VMEM((layers, 2, 2, rows, LANES), F32), pltpu.VMEM((2, 2, 2, rows, LANES), F32),
                             pltpu.VMEM((layers, half, 2, 8, LANES), F32), pltpu.VMEM((layers, 3, 2, half, LANES), F32),

time: 16.3 us -> 15.9 us (0.975)
  Pallas kernels: 15.5 us -> 15.1 us
    pallas_call x1, Pallas kernels: 14.8 us -> 14.5 us  [device_body(): pl.pallas_call(functools.partial(kernel, layers, total_bits, half, nqy),...]
where the time goes in v5:
time: 15.9 us; the launch traced here: 15.8 us
  Pallas kernels  15.1 us (95%)
  between operations  0.64 us (4%)
    pallas_call x1, Pallas kernels, device_body(): pl.pallas_call(functools.partial(kernel, layers, total_bits, half, nqy),...  14.5 us
    pallas_call x1, Pallas kernels, device_body(): pl.pallas_call(write_kernel, out_shape=(jax.ShapeDtypeStruct((1,), F32),...  0.64 us

profile of v5, /device:TPU:97, one launch (start us, length us, event | category | flops | bytes accessed | tf_op | source)
XLA Modules:
  0.0 15.8 jit_solution(3356518355379032865)
XLA Ops:
  0.6 14.5 %shard_map.58 = (f32[8,128]{1,0:T(8,128)S(1)}, f32[64,128]{1,0:T(8,128)S(1)}, f32[64,128]{1,0:T(8,128)S(1)}) custom-call(f32[4]{0:T(128)} %gamma_hbm.1, f32[4]{0:T(128)} %beta_hbm.1, f32[64,128]{1,0:T(8,128)} %bitcast.3), custom_call_target="tpu_custom_call" | custom-call | tf_op jit(solution)/shard_map/pallas_call | solution.py:370
  15.1 0.6 %shard_map.59 = (f32[1]{0:T(128)}, f32[64,128]{1,0:T(8,128)}, f32[64,128]{1,0:T(8,128)}) custom-call(f32[8,128]{1,0:T(8,128)S(1)} %get-tuple-element.9.partial_ref, f32[64,128]{1,0:T(8,128)S(1)} %get-tuple-element.10.re_in, f32[64,128]{1,0:T(8,128)S(1)} %get-tuple-element.11.im_in), custom_call_target="tpu_custom_call" | custom-call | tf_op jit(solution)/shard_map/pallas_call | solution.py:387

commit v6 on v5

--- a/solution.py
+++ b/solution.py
@@ -85,7 +85,7 @@
     return jnp.concatenate(blocks, axis=0)
 
 
-CHUNKS = ((0, 64, ((0, 64),)), (64, 64, ((64, 32), (96, 32))))
+CHUNKS = ((0, 64, ((0, 64),)), (64, 32, ()), (96, 32, ()))
 LAST_CHUNKS = ((0, 64, ((0, 64),)), (64, 64, ((64, 48), (112, 16))))
 
 
@@ -103,7 +103,7 @@
     near = nqy // 2
     hops = {e: (0, 1, 2, 1)[e // (2 * near)] + e % near for e in range(1, half)}
     asked = [e for e in hops if hops[e] < 2 or (hops[e] == 2 and (e // near) % 2 == 0)]
-    order = sorted(asked, key=lambda e: (-hops[e], e))
+    order = sorted(asked, key=lambda e: (-hops[e], -e))
     partners = {e: {'qx': flip_bits(me_x, e // near), 'qy': flip_bits(me_y, e % near)} for e in order}
     for e in order:
         pl.semaphore_signal(barrier, inc=1, device_id=partners[e], device_id_type=pl.DeviceIdType.MESH)
@@ -226,6 +226,9 @@
 
     def lanes_stage(l):
         for start, size, chunks in CHUNKS if l < layers - 1 else LAST_CHUNKS:
+            if not chunks:
+                yield start, size, mix_pairs(l, lanes_dot(l, (0, 3, 1, 2), start, size))
+                continue
             early = lanes_dot(l, (0, 3), start, size)
             for lo, n in chunks:
                 f = lanes_dot(l, (1, 2), lo, n)

time: 15.9 us -> 15.9 us (level)
  no operation moved by 1% of the time
where the time goes in v6:
time: 15.9 us; the launch traced here: 15.8 us
  Pallas kernels  15.1 us (95%)
  between operations  0.64 us (4%)
    pallas_call x1, Pallas kernels, device_body(): pl.pallas_call(functools.partial(kernel, layers, total_bits, half, nqy),...  14.5 us
    pallas_call x1, Pallas kernels, device_body(): pl.pallas_call(write_kernel, out_shape=(jax.ShapeDtypeStruct((1,), F32),...  0.64 us

profile of v6, /device:TPU:97, one launch (start us, length us, event | category | flops | bytes accessed | tf_op | source)
XLA Modules:
  0.0 15.8 jit_solution(11777685246879609117)
XLA Ops:
  0.6 14.5 %shard_map.58 = (f32[8,128]{1,0:T(8,128)S(1)}, f32[64,128]{1,0:T(8,128)S(1)}, f32[64,128]{1,0:T(8,128)S(1)}) custom-call(f32[4]{0:T(128)} %gamma_hbm.1, f32[4]{0:T(128)} %beta_hbm.1, f32[64,128]{1,0:T(8,128)} %bitcast.3), custom_call_target="tpu_custom_call" | custom-call | tf_op jit(solution)/shard_map/pallas_call | solution.py:373
  15.1 0.6 %shard_map.59 = (f32[1]{0:T(128)}, f32[64,128]{1,0:T(8,128)}, f32[64,128]{1,0:T(8,128)}) custom-call(f32[8,128]{1,0:T(8,128)S(1)} %get-tuple-element.9.partial_ref, f32[64,128]{1,0:T(8,128)S(1)} %get-tuple-element.10.re_in, f32[64,128]{1,0:T(8,128)S(1)} %get-tuple-element.11.im_in), custom_call_target="tpu_custom_call" | custom-call | tf_op jit(solution)/shard_map/pallas_call | solution.py:390

commit v7 on v6

--- a/solution.py
+++ b/solution.py
@@ -157,21 +157,17 @@
     bases = (cost, reverse_rows(cost))
     sub = lax.broadcasted_iota(jnp.int32, (8, LANES), 0)
 
-    def unit(turns):
-        co, si = turn_cos_sin(turns)
-        return co, -si
-
     def mul(x, y):
         return x[0] * y[0] - x[1] * y[1], x[0] * y[1] + x[1] * y[0]
 
-    rates = [gamma_ref[l] * (1.0 / (2.0 * math.pi)) for l in range(layers)]
+    rates = [gamma_ref[l] * (-1.0 / (2.0 * math.pi)) for l in range(layers)]
     for t in range(2):
         for l in range(1, layers):
-            for i, x in enumerate(unit(bases[t] * rates[l])):
+            for i, x in enumerate(turn_cos_sin(bases[t] * rates[l])):
                 base_ref[l, t, i] = x
         turns = bases[t] * rates[0]
-        turns = turns - jnp.round(turns) - quarter[:rows]
-        re, im = unit(turns)
+        turns = turns - jnp.round(turns) + quarter[:rows]
+        re, im = turn_cos_sin(turns)
         re, im = amp * re, amp * im
         for e0s, pair in enumerate(((re, im), (-im, re))):
             for i, x in enumerate(pair):
@@ -237,7 +233,7 @@
                 yield lo, n, mix_pairs(l, f)
 
     for e in order:
-        copies[e].wait()
+        copies[e].wait_recv()
     diff = {0: jnp.zeros((2, LANES), F32)}
     for e in order:
         diff[e] = table_ref[e] - own
@@ -257,10 +253,10 @@
 
     def put_factors(l):
         for k in range(3, row_bits):
-            for i, x in enumerate(unit(cols[k] * rates[l])):
+            for i, x in enumerate(turn_cos_sin(cols[k] * rates[l])):
                 high_ref[l, k - 3, i] = x
         for e in range(1, half):
-            for i, x in enumerate(unit(low[e] * rates[l])):
+            for i, x in enumerate(turn_cos_sin(low[e] * rates[l])):
                 low_ref[l, e, i] = x
 
     def factors(l, e):
@@ -348,6 +344,8 @@
             else:
                 put_cost(range(QUAD))
     energy_ref[...] = total
+    for e in order:
+        copies[e].wait_send()
 
 
 def write_kernel(partial_ref, re_in, im_in, energy_ref, re_ref, im_ref):

time: 15.9 us -> 15.9 us (level)
  no operation moved by 1% of the time
where the time goes in v7:
time: 15.9 us; the launch traced here: 15.8 us
  Pallas kernels  15.1 us (95%)
  between operations  0.64 us (4%)
    pallas_call x1, Pallas kernels, device_body(): pl.pallas_call(functools.partial(kernel, layers, total_bits, half, nqy),...  14.5 us
    pallas_call x1, Pallas kernels, device_body(): pl.pallas_call(write_kernel, out_shape=(jax.ShapeDtypeStruct((1,), F32),...  0.64 us

profile of v7, /device:TPU:97, one launch (start us, length us, event | category | flops | bytes accessed | tf_op | source)
XLA Modules:
  0.0 15.8 jit_solution(7357977916161860852)
XLA Ops:
  0.6 14.5 %shard_map.58 = (f32[8,128]{1,0:T(8,128)S(1)}, f32[64,128]{1,0:T(8,128)S(1)}, f32[64,128]{1,0:T(8,128)S(1)}) custom-call(f32[4]{0:T(128)} %gamma_hbm.1, f32[4]{0:T(128)} %beta_hbm.1, f32[64,128]{1,0:T(8,128)} %bitcast.3), custom_call_target="tpu_custom_call" | custom-call | tf_op jit(solution)/shard_map/pallas_call | solution.py:371
  15.1 0.6 %shard_map.59 = (f32[1]{0:T(128)}, f32[64,128]{1,0:T(8,128)}, f32[64,128]{1,0:T(8,128)}) custom-call(f32[8,128]{1,0:T(8,128)S(1)} %get-tuple-element.9.partial_ref, f32[64,128]{1,0:T(8,128)S(1)} %get-tuple-element.10.re_in, f32[64,128]{1,0:T(8,128)S(1)} %get-tuple-element.11.im_in), custom_call_target="tpu_custom_call" | custom-call | tf_op jit(solution)/shard_map/pallas_call | solution.py:388

commit v8 on v6

--- a/solution.py
+++ b/solution.py
@@ -86,7 +86,7 @@
 
 
 CHUNKS = ((0, 64, ((0, 64),)), (64, 32, ()), (96, 32, ()))
-LAST_CHUNKS = ((0, 64, ((0, 64),)), (64, 64, ((64, 48), (112, 16))))
+LAST_CHUNKS = ((0, 64, ((0, 64),)), (64, 48, ()), (112, 16, ()))
 
 
 def kernel(layers, total_bits, half, nqy, gamma_hbm, beta_hbm, cost_hbm, energy_ref, re_ref, im_ref,
@@ -178,8 +178,8 @@
                 start_ref[t, e0s, i] = x
 
     def place(e):
-        t = e // (2 * QUAD)
-        return t, e % QUAD, (e // QUAD) % 2 ^ t
+        t = e // 2 % 2
+        return t, e // 4, e % 2 ^ t
 
     def put_state(u, lo, x0, x1):
         n = x0.shape[0]
@@ -252,7 +252,7 @@
     for e in range(1, half):
         part = jnp.broadcast_to(first[e:e + 1, :], (8, LANES))
         for k in range(3):
-            part = part + jnp.where((sub // (1 << k)) % 2 == 1 - e // (2 * QUAD), cols[k][e:e + 1, :], 0.0)
+            part = part + jnp.where((sub // (1 << k)) % 2 == 1 - place(e)[0], cols[k][e:e + 1, :], 0.0)
         low[e] = part
 
     def put_factors(l):
@@ -268,7 +268,7 @@
         for k in range(row_bits - 3):
             h = (high_ref[l, k, 0, e:e + 1, :], high_ref[l, k, 1, e:e + 1, :])
             more = [mul(x, h) for x in out]
-            out = more + out if e // (2 * QUAD) else out + more
+            out = more + out if place(e)[0] else out + more
         return [jnp.concatenate([x[i] for x in out], axis=0) for i in range(2)]
 
     def put_phases(l, us):
@@ -299,7 +299,7 @@
     for u in (0, 3, 1, 2):
         xs = [[None, None], [None, None]]
         for e in range(half):
-            if e % QUAD == u:
+            if place(e)[1] == u:
                 t, _, e0s = place(e)
                 x = (start_ref[t, e0s, 0], start_ref[t, e0s, 1])
                 xs[t][e0s] = jnp.concatenate(mul(x, factors(0, e)) if e else x, axis=1)

time: 15.9 us -> 16 us (level)
  no operation moved by 1% of the time
where the time goes in v8:
time: 16 us; the launch traced here: 15.8 us
  Pallas kernels  15.2 us (95%)
  between operations  0.64 us (4%)
    pallas_call x1, Pallas kernels, device_body(): pl.pallas_call(functools.partial(kernel, layers, total_bits, half, nqy),...  14.6 us
    pallas_call x1, Pallas kernels, device_body(): pl.pallas_call(write_kernel, out_shape=(jax.ShapeDtypeStruct((1,), F32),...  0.64 us

profile of v8, /device:TPU:97, one launch (start us, length us, event | category | flops | bytes accessed | tf_op | source)
XLA Modules:
  0.0 15.8 jit_solution(16192842888998586974)
XLA Ops:
  0.6 14.6 %shard_map.58 = (f32[8,128]{1,0:T(8,128)S(1)}, f32[64,128]{1,0:T(8,128)S(1)}, f32[64,128]{1,0:T(8,128)S(1)}) custom-call(f32[4]{0:T(128)} %gamma_hbm.1, f32[4]{0:T(128)} %beta_hbm.1, f32[64,128]{1,0:T(8,128)} %bitcast.3), custom_call_target="tpu_custom_call" | custom-call | tf_op jit(solution)/shard_map/pallas_call | solution.py:373
  15.2 0.6 %shard_map.59 = (f32[1]{0:T(128)}, f32[64,128]{1,0:T(8,128)}, f32[64,128]{1,0:T(8,128)}) custom-call(f32[8,128]{1,0:T(8,128)S(1)} %get-tuple-element.9.partial_ref, f32[64,128]{1,0:T(8,128)S(1)} %get-tuple-element.10.re_in, f32[64,128]{1,0:T(8,128)S(1)} %get-tuple-element.11.im_in), custom_call_target="tpu_custom_call" | custom-call | tf_op jit(solution)/shard_map/pallas_call | solution.py:390
